TPU v7x, 32 devices: a whole 2x2x4 slice. The times are simulated.
32 devices in a mesh: rows: 16 (over z, y, x), feat: 2 (over core).
Axes of the slice: x: 2, y: 2, z: 4, core: 2. Of those that a mesh axis runs over, the one named last changes fastest.
Arguments:
- queries: bfloat16 [1024, 128], P('rows', 'feat'), may hold values from -6 to 6
- corpus: bfloat16 [524288, 128], P(('rows', 'feat')), as said below
- candidates: int32 [1024, 100], P(('rows', 'feat')), may hold values from 0 to 524287, as said below
- threshold: int32 [1024], replicated, may hold values from 100 to 199, as said below
Outputs:
- exceed: float32 [1024], P(('rows', 'feat'))
- candidate_scores: float32 [1024, 100], P(('rows', 'feat'))
Inputs may be any that keep to these rules, and one draw needn't show every extreme that they name: Passage ids. Of the 3200 candidates of one device's queries (aligned blocks of 32 rows), at most 100 lie in the 16384 passages of any one device, and exactly 100 in some device's. `corpus`: passage embeddings of order one or smaller; their scale differs between passages. Some query has threshold 100 and some 199.
All inputs are finite; a program needn't handle non-finite values.
Results may differ from a plain program's by a relative error of at most 0.00035.
Values may be sent and summed in bfloat16 or wider, within the bound.
A program may use at most 64 MiB of HBM per device.

v0:
```python
import jax
import jax.numpy as jnp
from jax import lax
from jax.sharding import PartitionSpec as P


def body(queries, corpus, candidates, threshold):
    rows_dev = corpus.shape[0]
    width = corpus.shape[1]
    shards = lax.axis_size("rows") * lax.axis_size("feat")
    owned_queries = candidates.shape[0]
    per_query = candidates.shape[1]
    npass_all = rows_dev * shards
    cutoff = threshold.astype(jnp.float32) * 0.01
    owner = lax.axis_index(("rows", "feat"))
    full_rows = lax.all_gather(queries, "feat", axis=1, tiled=True)
    whole = lax.all_gather(full_rows, "rows", axis=0, tiled=True)
    query_count = whole.shape[0]
    block = 2048
    corpus_blocks = corpus.reshape(rows_dev // block, block, width)

    def visit(total, block_rows):
        scores = lax.dot_general(
            whole, block_rows, (((1,), (1,)), ((), ())), preferred_element_type=jnp.float32
        )
        return (total + jnp.sum(jnp.maximum(scores - cutoff[:, None], 0.0), axis=1), None)

    total, _ = lax.scan(visit, jnp.zeros((query_count,), jnp.float32), corpus_blocks)
    flat_ids = candidates.reshape(-1)
    total_ids = flat_ids.shape[0]
    capacity = (total_ids + shards - 1) // shards
    target = flat_ids // rows_dev
    onehot = (target[:, None] == jnp.arange(shards, dtype=jnp.int32)[None, :]).astype(jnp.int32)
    before = jnp.cumsum(onehot, axis=0) - onehot
    rank = jnp.sum(before * onehot, axis=1)
    query_ids = owner * owned_queries + jnp.arange(total_ids, dtype=jnp.int32) // per_query
    fields = jnp.stack([flat_ids - target * rows_dev, query_ids], axis=1)
    send_both = jnp.zeros((shards, capacity, 2), jnp.int32).at[target, rank].set(fields)
    n_rows = lax.axis_size("rows")
    n_feat = lax.axis_size("feat")
    received = lax.all_to_all(
        lax.all_to_all(
            send_both.reshape(n_rows, n_feat, capacity * 2),
            "rows",
            split_axis=0,
            concat_axis=0,
            tiled=True,
        ),
        "feat",
        split_axis=1,
        concat_axis=1,
        tiled=True,
    )
    received = received.reshape(shards * capacity, 2)
    picked = corpus[received[:, 0]]
    asked = whole[received[:, 1]]
    values = jnp.einsum("kd,kd->k", picked, asked, preferred_element_type=jnp.float32).reshape(
        n_rows, n_feat, capacity
    )
    partials = total.reshape(n_rows, n_feat, owned_queries)
    answers, mass_parts = (
        lax.all_to_all(
            lax.all_to_all(values, "rows", split_axis=0, concat_axis=0, tiled=True),
            "feat",
            split_axis=1,
            concat_axis=1,
            tiled=True,
        ),
        lax.all_to_all(
            lax.all_to_all(partials, "rows", split_axis=0, concat_axis=0, tiled=True),
            "feat",
            split_axis=1,
            concat_axis=1,
            tiled=True,
        ),
    )
    exceed = jnp.sum(mass_parts, axis=(0, 1)) * (8.0 / npass_all)
    candidate_scores = answers.reshape(shards, capacity)[target, rank].reshape(
        owned_queries, per_query
    )
    return (exceed, candidate_scores)


def solution(mesh):
    return jax.shard_map(
        body,
        mesh=mesh,
        in_specs=(P("rows", "feat"), P(("rows", "feat"), None), P(("rows", "feat"), None), P()),
        out_specs=(P(("rows", "feat")), P(("rows", "feat"), None)),
        check_vma=False,
    )
```

profile of v0, /device:TPU:0, one launch (start us, length us, event | category | flops | bytes accessed | tf_op | source)
XLA Modules:
  0.0 177.3 jit_solution(1144586767254924828)
XLA Ops:
  1.4 2.0 %all_gather.6 = bf16[64,128]{0,1:T(8,128)(2,1)S(1)} all-gather(bf16[64,64]{0,1:T(8,128)(2,1)S(1)} %copy.40), channel_id=1, replica_groups=mesh['rows'=16,'feat'=2] {'feat'}, dimensions={1}, use_global_device_ids=true | all-gather | bytes 24576 | tf_op jit(solution)/shard_map/all_gather | solution.py:16
  3.5 43.7 %all_gather.7 = bf16[1024,128]{1,0:T(8,128)(2,1)S(1)} all-gather(bf16[64,128]{1,0:T(8,128)(2,1)S(1)} %copy.41), channel_id=1, replica_groups=mesh['rows'=16,'feat'=2] {'rows'}, dimensions={0}, use_global_device_ids=true | all-gather | bytes 278528 | tf_op jit(solution)/shard_map/all_gather | solution.py:17
  47.9 18.8 %while.11 = (s32[]{:T(128)}, f32[1024]{0:T(1024)S(1)}, bf16[8,2048,128]{2,1,0:T(8,128)(2,1)}, bf16[1024,128]{1,0:T(8,128)(2,1)S(1)}, f32[1024]{0:T(1024)S(1)}, /*index=5*/s32[]{:T(128)}, s32[]{:T(128)}) while((s32[]{:T(128)}, f32[1024]{0:T(1024)S(1)}, bf16[8,2048,128]{2,1,0:T(8,128)(2,1)}, bf16[1024,128]{1,0:T(8,128)(2,1)S(1)}, ...), condition=%wide.region_2.3_spmd.clone, body=%wide.region_0.2_spmd.clone.sunk | while | flops 543163392 | bytes 807511 | solution.py:28
  47.9 2.3 %maximum_reduce_fusion.2 = f32[1024]{0:T(1024)S(1)} fusion(bf16[1024,128]{1,0:T(8,128)(2,1)S(1)} %get-tuple-element.115, f32[1024]{0:T(1024)S(1)} %get-tuple-element.116, bf16[8,2048,128]{2,1,0:T(8,128)(2,1)} %get-tuple-element.114, s32[]{:T(128)} %get-tuple-element.105), kind=kOutput, calls=%fused_computation.4.clone.1 | convolution fusion | flops 543161344 | bytes 795136 | tf_op jit(solution)/shard_map/while/body/eval_jaxpr/dot_general | solution.py:23
  50.2 2.3 %maximum_reduce_fusion.2 = f32[1024]{0:T(1024)S(1)} fusion(bf16[1024,128]{1,0:T(8,128)(2,1)S(1)} %get-tuple-element.115, f32[1024]{0:T(1024)S(1)} %get-tuple-element.116, bf16[8,2048,128]{2,1,0:T(8,128)(2,1)} %get-tuple-element.114, s32[]{:T(128)} %get-tuple-element.105), kind=kOutput, calls=%fused_computation.4.clone.1 | convolution fusion | flops 543161344 | bytes 795136 | tf_op jit(solution)/shard_map/while/body/eval_jaxpr/dot_general | solution.py:23
  52.6 2.3 %maximum_reduce_fusion.2 = f32[1024]{0:T(1024)S(1)} fusion(bf16[1024,128]{1,0:T(8,128)(2,1)S(1)} %get-tuple-element.115, f32[1024]{0:T(1024)S(1)} %get-tuple-element.116, bf16[8,2048,128]{2,1,0:T(8,128)(2,1)} %get-tuple-element.114, s32[]{:T(128)} %get-tuple-element.105), kind=kOutput, calls=%fused_computation.4.clone.1 | convolution fusion | flops 543161344 | bytes 795136 | tf_op jit(solution)/shard_map/while/body/eval_jaxpr/dot_general | solution.py:23
  54.9 2.3 %maximum_reduce_fusion.2 = f32[1024]{0:T(1024)S(1)} fusion(bf16[1024,128]{1,0:T(8,128)(2,1)S(1)} %get-tuple-element.115, f32[1024]{0:T(1024)S(1)} %get-tuple-element.116, bf16[8,2048,128]{2,1,0:T(8,128)(2,1)} %get-tuple-element.114, s32[]{:T(128)} %get-tuple-element.105), kind=kOutput, calls=%fused_computation.4.clone.1 | convolution fusion | flops 543161344 | bytes 795136 | tf_op jit(solution)/shard_map/while/body/eval_jaxpr/dot_general | solution.py:23
  57.3 2.3 %maximum_reduce_fusion.2 = f32[1024]{0:T(1024)S(1)} fusion(bf16[1024,128]{1,0:T(8,128)(2,1)S(1)} %get-tuple-element.115, f32[1024]{0:T(1024)S(1)} %get-tuple-element.116, bf16[8,2048,128]{2,1,0:T(8,128)(2,1)} %get-tuple-element.114, s32[]{:T(128)} %get-tuple-element.105), kind=kOutput, calls=%fused_computation.4.clone.1 | convolution fusion | flops 543161344 | bytes 795136 | tf_op jit(solution)/shard_map/while/body/eval_jaxpr/dot_general | solution.py:23
  59.6 2.3 %maximum_reduce_fusion.2 = f32[1024]{0:T(1024)S(1)} fusion(bf16[1024,128]{1,0:T(8,128)(2,1)S(1)} %get-tuple-element.115, f32[1024]{0:T(1024)S(1)} %get-tuple-element.116, bf16[8,2048,128]{2,1,0:T(8,128)(2,1)} %get-tuple-element.114, s32[]{:T(128)} %get-tuple-element.105), kind=kOutput, calls=%fused_computation.4.clone.1 | convolution fusion | flops 543161344 | bytes 795136 | tf_op jit(solution)/shard_map/while/body/eval_jaxpr/dot_general | solution.py:23
  62.0 2.3 %maximum_reduce_fusion.2 = f32[1024]{0:T(1024)S(1)} fusion(bf16[1024,128]{1,0:T(8,128)(2,1)S(1)} %get-tuple-element.115, f32[1024]{0:T(1024)S(1)} %get-tuple-element.116, bf16[8,2048,128]{2,1,0:T(8,128)(2,1)} %get-tuple-element.114, s32[]{:T(128)} %get-tuple-element.105), kind=kOutput, calls=%fused_computation.4.clone.1 | convolution fusion | flops 543161344 | bytes 795136 | tf_op jit(solution)/shard_map/while/body/eval_jaxpr/dot_general | solution.py:23
  64.3 2.3 %maximum_reduce_fusion.2 = f32[1024]{0:T(1024)S(1)} fusion(bf16[1024,128]{1,0:T(8,128)(2,1)S(1)} %get-tuple-element.115, f32[1024]{0:T(1024)S(1)} %get-tuple-element.116, bf16[8,2048,128]{2,1,0:T(8,128)(2,1)} %get-tuple-element.114, s32[]{:T(128)} %get-tuple-element.105), kind=kOutput, calls=%fused_computation.4.clone.1 | convolution fusion | flops 543161344 | bytes 795136 | tf_op jit(solution)/shard_map/while/body/eval_jaxpr/dot_general | solution.py:23
  67.3 4.1 %all-to-all-start = ((f32[16,2,32]{2,1,0:T(2,128)}), f32[16,2,32]{2,1,0:T(2,128)}, u32[]{:S(2)}, u32[]{:S(2)}) async-start(f32[16,2,32]{2,1,0:T(2,128)} %reshape.217), calls=%async_computation | async-start | bytes 32768 | tf_op jit(solution)/shard_map/all_to_all | solution.py:70
  71.9 9.2 %reduce-window.6 = s32[32,25,128]{2,1,0:T(8,128)S(1)} reduce-window(s32[32,25,128]{2,1,0:T(8,128)S(1)} %fusion.6, s32[]{:T(128)} %constant.28.clone.1), window={size=1x1x128 pad=0_0x0_0x127_0}, to_apply=%region_4.5 | reduce-window | flops 13004800 | bytes 819204 | tf_op jit(solution)/shard_map/reduce-window
  84.2 13.8 %scatter_custom_fusion = s32[3200,2]{1,0:T(8,128)S(1)} fusion(s32[3200]{0:T(1024)} %broadcast_select_fusion, s32[3200,2]{1,0:T(8,128)S(1)} %copy.44, s32[]{:T(128)} %constant.28.clone.1), kind=kCustom, calls=%fused_computation.11 | custom fusion | bytes 26112
  100.2 3.7 %all_to_all.30 = f32[2,1,512]{2,1,0:T(1,128)S(1)} all-to-all(f32[2,1,512]{2,1,0:T(1,128)S(1)} %reshape.269), channel_id=1, replica_groups=mesh['rows'=16,'feat'=2] {'feat'}, dimensions={0} | all-to-all | bytes 8192 | tf_op jit(solution)/shard_map/all_to_all | solution.py:69
  103.8 6.8 %all-to-all-start.2 = ((s32[16,2,200]{2,1,0:T(2,128)}), s32[16,2,200]{2,1,0:T(2,128)S(1)}, u32[]{:S(2)}, u32[]{:S(2)}) async-start(s32[16,2,200]{2,1,0:T(2,128)} %reshape.222), calls=%async_computation.2 | async-start | bytes 65536 | tf_op jit(solution)/shard_map/all_to_all | solution.py:42
  112.5 5.6 %all-to-all-done.2 = s32[16,2,200]{2,1,0:T(2,128)S(1)} async-done(((s32[16,2,200]{2,1,0:T(2,128)}), s32[16,2,200]{2,1,0:T(2,128)S(1)}, u32[]{:S(2)}, u32[]{:S(2)}) %all-to-all-start.2) | async-done | bytes 25632 | tf_op jit(solution)/shard_map/all_to_all | solution.py:42
  118.1 3.7 %all_to_all.31 = s32[16,2,200]{2,0,1:T(8,128)S(1)} all-to-all(s32[16,2,200]{2,0,1:T(8,128)S(1)} %copy.45), channel_id=1, replica_groups=mesh['rows'=16,'feat'=2] {'feat'}, dimensions={1} | all-to-all | bytes 51200 | tf_op jit(solution)/shard_map/all_to_all | solution.py:41
  126.0 6.7 %gather_fusion.1 = bf16[3200,128]{1,0:T(8,128)(2,1)S(1)} fusion(bf16[1024,128]{1,0:T(8,128)(2,1)S(1)} %get-tuple-element.119, s32[4096]{0:T(1024)S(1)} %pad_clamp_fusion), kind=kCustom, calls=%fused_computation.1 | custom fusion | bytes 1651200 | tf_op jit(solution)/shard_map/gather | solution.py:56
  133.3 8.5 %gather_fusion = bf16[3200,128]{1,0:T(8,128)(2,1)S(1)} fusion(bf16[16384,128]{1,0:T(8,128)(2,1)} %bitcast.35, s32[4096]{0:T(1024)S(1)} %pad_clamp_fusion.1), kind=kCustom, calls=%fused_computation | custom fusion | bytes 1651200 | tf_op jit(solution)/shard_map/gather | solution.py:55
  143.1 3.5 %all-to-all-start.4 = ((f32[16,2,100]{2,1,0:T(2,128)}), f32[16,2,100]{2,1,0:T(2,128)S(1)}, u32[]{:S(2)}, u32[]{:S(2)}) async-start(f32[16,2,100]{2,1,0:T(2,128)} %reshape.224), calls=%async_computation.4 | async-start | bytes 32768 | tf_op jit(solution)/shard_map/all_to_all | solution.py:63
  147.1 6.8 %all-to-all-done.4 = f32[16,2,100]{2,1,0:T(2,128)S(1)} async-done(((f32[16,2,100]{2,1,0:T(2,128)}), f32[16,2,100]{2,1,0:T(2,128)S(1)}, u32[]{:S(2)}, u32[]{:S(2)}) %all-to-all-start.4) | async-done | bytes 12832 | tf_op jit(solution)/shard_map/all_to_all | solution.py:63
  153.9 3.7 %all_to_all.32 = f32[16,2,100]{2,0,1:T(8,128)S(1)} all-to-all(f32[16,2,100]{2,0,1:T(8,128)S(1)} %copy.49), channel_id=1, replica_groups=mesh['rows'=16,'feat'=2] {'feat'}, dimensions={1} | all-to-all | bytes 25600 | tf_op jit(solution)/shard_map/all_to_all | solution.py:62
  157.6 19.0 %gather_fusion.2 = f32[3200]{0:T(1024)S(1)} fusion(f32[32,100]{1,0:T(8,128)S(1)} %bitcast.33, s32[3200]{0:T(1024)S(1)} %get-tuple-element.58), kind=kCustom, calls=%fused_computation.2 | custom fusion | bytes 51200 | tf_op jit(solution)/shard_map/gather | solution.py:78
  (62 shorter events, 16.9 us)
Async XLA Ops:
  47.9 23.6 %copy-start = (s32[32,100]{1,0:T(8,128)S(1)}, s32[32,100]{1,0:T(8,128)}, u32[]{:S(2)}) copy-start(s32[32,100]{1,0:T(8,128)} %param.8) | copy-start | bytes 38404
  67.3 32.0 %all-to-all-start = ((f32[16,2,32]{2,1,0:T(2,128)}), f32[16,2,32]{2,1,0:T(2,128)}, u32[]{:S(2)}, u32[]{:S(2)}) async-start(f32[16,2,32]{2,1,0:T(2,128)} %reshape.217), calls=%async_computation | async-start | bytes 32768 | tf_op jit(solution)/shard_map/all_to_all | solution.py:70
  71.9 11.0 %copy-start.2 = (s32[2]{0:T(128)S(1)}, s32[2]{0:T(128)}, u32[]{:S(2)}) copy-start(s32[2]{0:T(128)} %constant.67) | copy-start | bytes 28
  71.9 11.1 %copy-start.1 = (s32[2]{0:T(128)S(1)}, s32[2]{0:T(128)}, u32[]{:S(2)}) copy-start(s32[2]{0:T(128)} %constant.64) | copy-start | bytes 28
  103.8 14.2 %all-to-all-start.2 = ((s32[16,2,200]{2,1,0:T(2,128)}), s32[16,2,200]{2,1,0:T(2,128)S(1)}, u32[]{:S(2)}, u32[]{:S(2)}) async-start(s32[16,2,200]{2,1,0:T(2,128)} %reshape.222), calls=%async_computation.2 | async-start | bytes 65536 | tf_op jit(solution)/shard_map/all_to_all | solution.py:42
  141.8 4.8 %copy-start.3 = (f32[32]{0:T(128)S(1)}, f32[32]{0:T(128)}, u32[]{:S(2)}) copy-start(f32[32]{0:T(128)} %bitcast_reduce_fusion) | copy-start | bytes 388
  143.1 10.8 %all-to-all-start.4 = ((f32[16,2,100]{2,1,0:T(2,128)}), f32[16,2,100]{2,1,0:T(2,128)S(1)}, u32[]{:S(2)}, u32[]{:S(2)}) async-start(f32[16,2,100]{2,1,0:T(2,128)} %reshape.224), calls=%async_computation.4 | async-start | bytes 32768 | tf_op jit(solution)/shard_map/all_to_all | solution.py:63
where the time goes:
time: 178 us; the launch traced here: 177 us
  local copies, waits for them, and re-layouts  59.9 us (34%)
  blocking collectives  56.8 us (32%)
  matrix products  18.5 us (10%)
  starting transfers between devices  14.4 us (8%)
  other arithmetic  14.1 us (8%)
  waiting for transfers between devices  12.4 us (7%)
    all_gather x1, blocking collectives, body(): whole = lax.all_gather(full_rows, 'rows', axis=0, tiled=True)  43.7 us
    gather x1, local copies, waits for them, and re-layouts, body(): answers.reshape(shards, capacity)[target, rank]  19 us
    dot_general x8, matrix products, visit(): lax.dot_general(whole, block_rows, (((1,), (1,)), ((), ())), preferred_el...  18.5 us
    unnamed x14, local copies, waits for them, and re-layouts  17.2 us
    another operation x3, other arithmetic  9.61 us
    gather x1, local copies, waits for them, and re-layouts, body(): picked = corpus[received[:, 0]]  8.48 us
    all_to_all x1, starting transfers between devices, body(): lax.all_to_all(send_both.reshape(n_rows, n_feat, capacity * 2), 'rows', s...  6.81 us
    all_to_all x1, waiting for transfers between devices, body(): lax.all_to_all(values, 'rows', split_axis=0, concat_axis=0, tiled=True)  6.78 us
  transfers between devices with their start and end apart: 3, of which 2 were waited for; matrix products, arithmetic and copies ran while one was open for 17% of the time, Pallas kernels for 0%

commit v1 on v0

--- a/solution.py
+++ b/solution.py
@@ -1,10 +1,272 @@
+import functools
+
 import jax
 import jax.numpy as jnp
 from jax import lax
+from jax.experimental import pallas as pl
+from jax.experimental.pallas import tpu as pltpu
 from jax.sharding import PartitionSpec as P
 
-
-def body(queries, corpus, candidates, threshold):
+LANES = 128
+TILE = 256
+BLOCK = 512
+MESH = pl.DeviceIdType.MESH
+
+
+def bulk_wait(ref, sem):
+    pltpu.make_async_copy(ref, ref, sem).wait()
+
+
+def kernel(
+    n, nf, npass_all, capacity,
+    q_ref, thr_ref, cand_ref, corpus_ref,
+    mass_out, ans_out,
+    corpus_v, corpus_f, q_pack, q_in, q_full, cand_pad, ranks, places,
+    ids_out, ids_in, ids_sm, rows_v, vals_out, vals_in, mass_rows, mass_in,
+    load_sem, sm_sem, q_send, q_recv, ids_send, ids_recv, vals_send, vals_recv, mass_send, mass_recv,
+):
+    rows_dev, width = corpus_v.shape
+    owned, per_query = cand_ref.shape
+    nq = q_full.shape[0]
+    half = q_ref.shape[1]
+    tiles = nq // TILE
+    dpt = TILE // owned
+    me = lax.axis_index("rows") * nf + lax.axis_index("feat")
+    my_tile = me // dpt
+    my_j = me % dpt
+    id_bits = rows_dev.bit_length() - 1
+
+    load = pltpu.make_async_copy(corpus_ref, corpus_v, load_sem)
+    load.start()
+
+    def tile_at(i):
+        return (my_tile + i) % tiles
+
+    def peers(i, act):
+        def step(j, carry):
+            act(tile_at(i) * dpt + (my_j + j) % dpt)
+            return carry
+        lax.fori_loop(1 if i == 0 else 0, dpt, step, 0)
+
+    def where_is(d):
+        return (d // nf, d % nf)
+
+    barrier = pltpu.get_barrier_semaphore()
+    for i in range(tiles):
+        peers(i, lambda d: pl.semaphore_signal(
+            barrier, inc=1, device_id=where_is(d), device_id_type=MESH))
+
+    q_local = q_ref[...].astype(jnp.float32)
+    mine = jnp.concatenate([q_local[:owned], q_local[owned:]], axis=1).astype(jnp.bfloat16)
+    q_pack[...] = mine
+    q_in[me] = mine
+
+    cand_pad[...] = jnp.full(cand_pad.shape, -1, jnp.int32)
+    cand_pad[:, :per_query] = cand_ref[...]
+    cand = cand_pad[...]
+    target = lax.shift_right_arithmetic(cand, jnp.int32(id_bits))
+    local = jnp.bitwise_and(cand, jnp.int32(rows_dev - 1))
+    low = jnp.bitwise_and(local, jnp.int32(LANES - 1)).astype(jnp.float32)
+    high = lax.shift_right_arithmetic(local, jnp.int32(7)).astype(jnp.float32)
+    dest = lax.broadcasted_iota(jnp.int32, (n, LANES), 0)
+    hot = [jnp.where(target[q:q + 1] == dest, 1.0, 0.0) for q in range(owned)]
+    row_i = lax.broadcasted_iota(jnp.int32, (LANES, 2 * LANES), 0)
+    col_i = lax.broadcasted_iota(jnp.int32, (LANES, 2 * LANES), 1)
+    upper = jnp.where((row_i < col_i) | (col_i >= LANES), 1.0, 0.0).astype(jnp.bfloat16)
+    counts = jnp.dot(
+        jnp.concatenate(hot, axis=0).astype(jnp.bfloat16), upper, preferred_element_type=jnp.float32)
+    base = jnp.zeros((n, LANES), jnp.float32)
+    slot = lax.broadcasted_iota(jnp.int32, (LANES, LANES), 0).astype(jnp.float32)
+    fields = []
+    for q in range(owned):
+        block = counts[q * n:(q + 1) * n]
+        rank = jnp.sum(hot[q] * (block[:, :LANES] + base), axis=0, keepdims=True)
+        base = base + block[:, LANES:]
+        places[:, q * LANES:(q + 1) * LANES] = jnp.where(rank == slot, 1.0, 0.0).astype(jnp.bfloat16)
+        fields.append(jnp.concatenate(
+            [hot[q] * low[q:q + 1], hot[q] * high[q:q + 1], hot[q] * float(q)], axis=0
+        ).astype(jnp.bfloat16))
+    sorted_fields = lax.dot_general(
+        jnp.concatenate(fields, axis=1), places[...], (((1,), (1,)), ((), ())),
+        preferred_element_type=jnp.float32)
+    packed = (
+        sorted_fields[:n] + sorted_fields[n:2 * n] * float(LANES) + sorted_fields[2 * n:] * float(rows_dev)
+    ).astype(jnp.int32)
+    for t in range(n):
+        ids_out[t] = packed[t:t + 1]
+
+    pl.semaphore_wait(barrier, n - 1)
+
+    for i in range(tiles):
+        def send_queries(d):
+            pltpu.make_async_remote_copy(
+                src_ref=q_pack, dst_ref=q_in.at[me], send_sem=q_send, recv_sem=q_recv.at[my_tile],
+                device_id=where_is(d), device_id_type=MESH).start()
+        peers(i, send_queries)
+    for i in range(tiles):
+        def send_ids(d):
+            pltpu.make_async_remote_copy(
+                src_ref=ids_out.at[d], dst_ref=ids_in.at[me], send_sem=ids_send, recv_sem=ids_recv,
+                device_id=where_is(d), device_id_type=MESH).start()
+        peers(i, send_ids)
+    ids_in[me] = ids_out[me]
+
+    load.wait()
+
+    def widen(b, carry):
+        at = pl.ds(pl.multiple_of(b * BLOCK, BLOCK), BLOCK)
+        corpus_f[at, :] = corpus_v[at, :].astype(jnp.float32)
+        return carry
+    lax.fori_loop(0, rows_dev // BLOCK, widen, 0)
+
+    left = lax.broadcasted_iota(jnp.int32, (owned, LANES), 1) < half
+    to_smem = pltpu.make_async_copy(ids_in, ids_sm, sm_sem)
+    blocks = rows_dev // BLOCK
+    for i in range(tiles):
+        tile = tile_at(i)
+        if i == 0:
+            bulk_wait(q_in.at[pl.ds(0, dpt - 1)], q_recv.at[tile])
+        else:
+            bulk_wait(q_in.at[pl.ds(0, dpt)], q_recv.at[tile])
+        parts = []
+        for g in range(dpt // 2):
+            f0 = q_in[tile * dpt + 2 * g].astype(jnp.float32)
+            f1 = q_in[tile * dpt + 2 * g + 1].astype(jnp.float32)
+            parts.append(jnp.where(left, f0, pltpu.roll(f1, half, 1)))
+            parts.append(jnp.where(left, pltpu.roll(f0, half, 1), f1))
+        asked = jnp.concatenate(parts, axis=0)
+        start = pl.multiple_of(tile * TILE, TILE)
+        q_full[pl.ds(start, TILE), :] = asked.astype(jnp.bfloat16)
+        weights = asked.T.astype(jnp.bfloat16)
+        cutoff = thr_ref[:, pl.ds(start, TILE)].astype(jnp.float32) * 0.01
+        if i == tiles - 2:
+            bulk_wait(ids_in.at[pl.ds(0, n - 1)], ids_recv)
+            to_smem.start()
+            to_smem.wait()
+
+        def sweep(b, acc):
+            at = pl.ds(pl.multiple_of(b * BLOCK, BLOCK), BLOCK)
+            scores = jnp.dot(corpus_v[at, :], weights, preferred_element_type=jnp.float32)
+            over = jnp.maximum(scores - cutoff, 0.0)
+            if i == tiles - 2:
+                for r in range(capacity):
+                    p = jnp.bitwise_and(ids_sm[b, 0, r], rows_dev - 1)
+                    rows_v[b, pl.ds(r, 1), :] = corpus_f[pl.ds(p, 1), :]
+            if i == tiles - 1:
+                pairs = lax.dot_general(
+                    q_full[pl.ds(pl.multiple_of(b * owned, owned), owned), :],
+                    rows_v[b].astype(jnp.bfloat16),
+                    (((1,), (1,)), ((), ())), preferred_element_type=jnp.float32)
+                who = lax.shift_right_arithmetic(ids_in[b], jnp.int32(id_bits))
+                mask = (who == lax.broadcasted_iota(jnp.int32, (owned, LANES), 0)) & (
+                    lax.broadcasted_iota(jnp.int32, (owned, LANES), 1) < capacity)
+                vals_out[b] = jnp.sum(jnp.where(mask, pairs, 0.0), axis=0, keepdims=True)
+            return acc + jnp.sum(over.reshape(BLOCK // 8, 8, TILE), axis=0)
+
+        acc = lax.fori_loop(0, blocks, sweep, jnp.zeros((8, TILE), jnp.float32))
+        total = jnp.sum(acc, axis=0, keepdims=True)
+        for h in range(TILE // LANES):
+            mass_rows[tile * (TILE // LANES) + h] = total[:, h * LANES:(h + 1) * LANES]
+
+        def send_mass(d):
+            pltpu.make_async_remote_copy(
+                src_ref=mass_rows.at[d * owned // LANES], dst_ref=mass_in.at[me],
+                send_sem=mass_send, recv_sem=mass_recv,
+                device_id=where_is(d), device_id_type=MESH).start()
+        peers(i, send_mass)
+        if i == 0:
+            mass_in[me] = mass_rows[me * owned // LANES]
+
+    for i in range(tiles):
+        def send_vals(d):
+            pltpu.make_async_remote_copy(
+                src_ref=vals_out.at[d], dst_ref=vals_in.at[me], send_sem=vals_send, recv_sem=vals_recv,
+                device_id=where_is(d), device_id_type=MESH).start()
+        peers(i, send_vals)
+    vals_in[me] = vals_out[me]
+
+    bulk_wait(vals_in.at[pl.ds(0, n - 1)], vals_recv)
+    values = jnp.concatenate([vals_in[t] for t in range(n)], axis=0)
+    top = values.astype(jnp.bfloat16)
+    rest = values - top.astype(jnp.float32)
+    mid = rest.astype(jnp.bfloat16)
+    last = (rest - mid.astype(jnp.float32)).astype(jnp.bfloat16)
+    pieces = jnp.concatenate([top, mid, last], axis=0)
+    cand = cand_pad[...]
+    target = lax.shift_right_arithmetic(cand, jnp.int32(id_bits))
+    for q in range(owned):
+        spread = jnp.dot(
+            pieces, places[:, q * LANES:(q + 1) * LANES], preferred_element_type=jnp.float32)
+        spread = (spread[2 * n:] + spread[n:2 * n]) + spread[:n]
+        ans_out[q:q + 1, :] = jnp.sum(
+            jnp.where(target[q:q + 1] == dest, spread, 0.0), axis=0, keepdims=True)
+
+    bulk_wait(mass_in.at[pl.ds(0, n - 1)], mass_recv)
+    mass = mass_in[0]
+    for t in range(1, n):
+        mass = mass + mass_in[t]
+    mass = mass * (8.0 / npass_all)
+    per_row = LANES // owned
+    result = mass
+    for u in range(1, per_row):
+        result = jnp.where(me % per_row == u, pltpu.roll(mass, LANES - u * owned, 1), result)
+    mass_out[...] = result
+
+    bulk_wait(q_in.at[pl.ds(0, n - 1)], q_send)
+    bulk_wait(ids_in.at[pl.ds(0, n - 1)], ids_send)
+    bulk_wait(vals_in.at[pl.ds(0, n - 1)], vals_send)
+    bulk_wait(mass_in.at[pl.ds(0, n - 1)], mass_send)
+
+
+def fused_body(n, nf, queries, corpus, candidates, threshold):
+    rows_dev, width = corpus.shape
+    owned, per_query = candidates.shape
+    nq = n * owned
+    capacity = (owned * per_query + n - 1) // n
+    vmem = pl.BlockSpec(memory_space=pltpu.VMEM)
+    mass, answers = pl.pallas_call(
+        functools.partial(kernel, n, nf, rows_dev * n, capacity),
+        out_shape=(
+            jax.ShapeDtypeStruct((1, LANES), jnp.float32),
+            jax.ShapeDtypeStruct((owned, LANES), jnp.float32),
+        ),
+        in_specs=[vmem, vmem, vmem, pl.BlockSpec(memory_space=pl.ANY)],
+        out_specs=(vmem, vmem),
+        scratch_shapes=[
+            pltpu.VMEM((rows_dev, width), jnp.bfloat16),
+            pltpu.VMEM((rows_dev, width), jnp.float32),
+            pltpu.VMEM((owned, LANES), jnp.bfloat16),
+            pltpu.VMEM((n, owned, LANES), jnp.bfloat16),
+            pltpu.VMEM((nq, LANES), jnp.bfloat16),
+            pltpu.VMEM((owned, LANES), jnp.int32),
+            pltpu.VMEM((owned, LANES), jnp.float32),
+            pltpu.VMEM((LANES, owned * LANES), jnp.bfloat16),
+            pltpu.VMEM((n, 1, LANES), jnp.int32),
+            pltpu.VMEM((n, 1, LANES), jnp.int32),
+            pltpu.SMEM((n, 1, LANES), jnp.int32),
+            pltpu.VMEM((n, LANES, LANES), jnp.float32),
+            pltpu.VMEM((n, 1, LANES), jnp.float32),
+            pltpu.VMEM((n, 1, LANES), jnp.float32),
+            pltpu.VMEM((nq // LANES, 1, LANES), jnp.float32),
+            pltpu.VMEM((n, 1, LANES), jnp.float32),
+            pltpu.SemaphoreType.DMA,
+            pltpu.SemaphoreType.DMA,
+            pltpu.SemaphoreType.DMA,
+            pltpu.SemaphoreType.DMA((nq // TILE,)),
+            pltpu.SemaphoreType.DMA,
+            pltpu.SemaphoreType.DMA,
+            pltpu.SemaphoreType.DMA,
+            pltpu.SemaphoreType.DMA,
+            pltpu.SemaphoreType.DMA,
+            pltpu.SemaphoreType.DMA,
+        ],
+        compiler_params=pltpu.CompilerParams(
+            collective_id=0, has_side_effects=True, vmem_limit_bytes=48 * 1024 * 1024),
+    )(queries, threshold.reshape(1, nq), candidates, corpus)
+    return mass[0, :owned], answers[:, :per_query]
+
+
+def plain_body(queries, corpus, candidates, threshold):
     rows_dev = corpus.shape[0]
     width = corpus.shape[1]
     shards = lax.axis_size("rows") * lax.axis_size("feat")
@@ -81,6 +343,31 @@
     return (exceed, candidate_scores)
 
 
+def body(queries, corpus, candidates, threshold):
+    nf = lax.axis_size("feat")
+    n = lax.axis_size("rows") * nf
+    rows_dev, width = corpus.shape
+    owned, per_query = candidates.shape
+    capacity = (owned * per_query + n - 1) // n
+    fits = (
+        nf == 2
+        and width == LANES
+        and queries.shape == (2 * owned, LANES // 2)
+        and owned % 32 == 0
+        and LANES % owned == 0
+        and per_query <= LANES
+        and capacity <= LANES
+        and n % 8 == 0
+        and (n * owned) % TILE == 0
+        and n * owned >= 2 * TILE
+        and rows_dev == n * BLOCK
+        and rows_dev & (rows_dev - 1) == 0
+    )
+    if fits:
+        return fused_body(n, nf, queries, corpus, candidates, threshold)
+    return plain_body(queries, corpus, candidates, threshold)
+
+
 def solution(mesh):
     return jax.shard_map(
         body,

time: 178 us -> 56 us (0.31)
  blocking collectives: 56.8 us -> 0 us
  local copies, waits for them, and re-layouts: 59.9 us -> 5.42 us
  Pallas kernels: 0 us -> 49.6 us
  matrix products: 18.5 us -> 0 us
  starting transfers between devices: 14.4 us -> 0 us
  other arithmetic: 14.1 us -> 0 us
  waiting for transfers between devices: 12.4 us -> 0 us
    pallas_call x0 -> x1, Pallas kernels: none -> 49.6 us  [fused_body(): pl.pallas_call(functools.partial(kernel, n, nf, rows_dev * n, capacity),...]
    all_gather x2 -> x0, blocking collectives: 45.6 us -> none  [the longest x1 43.7 us: body(): whole = lax.all_gather(full_rows, 'rows', axis=0, tiled=True)]
    gather x3 -> x0, local copies, waits for them, and re-layouts: 34.2 us -> none  [the longest x1 19 us: body(): answers.reshape(shards, capacity)[target, rank]]
    dot_general x8 -> x0, matrix products: 18.5 us -> none  [visit(): lax.dot_general(whole, block_rows, (((1,), (1,)), ((), ())), preferred_el...]
    all_to_all x3 -> x0, starting transfers between devices: 14.4 us -> none  [the longest x1 6.81 us: body(): lax.all_to_all(send_both.reshape(n_rows, n_feat, capacity * 2), 'rows', s...]
    all_to_all x3 -> x0, waiting for transfers between devices: 12.4 us -> none  [the longest x1 6.78 us: body(): lax.all_to_all(values, 'rows', split_axis=0, concat_axis=0, tiled=True)]
    unnamed x14 -> x9, local copies, waits for them, and re-layouts: 17.2 us -> 4.91 us
    all_to_all x3 -> x0, blocking collectives: 11.1 us -> none  [the longest x1 3.73 us: body(): lax.all_to_all(lax.all_to_all(send_both.reshape(n_rows, n_feat, capacity...]
  transfers between devices with their start and end apart: 3 -> 0, of which waited for: 2 -> 0; matrix products, arithmetic and copies ran while one was open for 17% -> 0% of each run, Pallas kernels for 0% -> 0%
where the time goes in v1:
time: 56 us; the launch traced here: 55.7 us
  Pallas kernels  49.6 us (89%)
  local copies, waits for them, and re-layouts  5.42 us (10%)
  between operations  0.65 us (1%)
    pallas_call x1, Pallas kernels, fused_body(): pl.pallas_call(functools.partial(kernel, n, nf, rows_dev * n, capacity),...  49.6 us
    unnamed x9, local copies, waits for them, and re-layouts  4.91 us

profile of v1, /device:TPU:0, one launch (start us, length us, event | category | flops | bytes accessed | tf_op | source)
XLA Modules:
  0.0 55.7 jit_solution(6933985111813678872)
XLA Ops:
  0.6 0.0 copy-start
  0.6 2.2 %copy-done = bf16[16384,128]{1,0:T(8,128)(2,1)S(1)} copy-done((bf16[16384,128]{1,0:T(8,128)(2,1)S(1)}, bf16[16384,128]{1,0:T(8,128)(2,1)}, u32[]{:S(2)}) %copy-start) | copy-done | bytes 4194328
  2.8 0.0 copy-start.1
  2.8 0.7 %copy-done.1 = bf16[64,64]{1,0:T(8,128)(2,1)S(1)} copy-done((bf16[64,64]{1,0:T(8,128)(2,1)S(1)}, bf16[64,64]{1,0:T(8,128)(2,1)}, u32[]{:S(2)}) %copy-start.1) | copy-done | bytes 8216
  3.5 0.0 copy-start.2
  3.5 0.7 %copy-done.2 = s32[32,100]{1,0:T(8,128)S(1)} copy-done((s32[32,100]{1,0:T(8,128)S(1)}, s32[32,100]{1,0:T(8,128)}, u32[]{:S(2)}) %copy-start.2) | copy-done | bytes 12824
  4.3 0.0 copy-start.3
  4.3 0.7 %copy-done.3 = s32[1024]{0:T(1024)S(1)} copy-done((s32[1024]{0:T(1024)S(1)}, s32[1024]{0:T(1024)}, u32[]{:S(2)}) %copy-start.3) | copy-done | bytes 4120
  4.9 49.6 %shard_map.59 = (f32[1,128]{1,0:T(1,128)S(1)}, f32[32,128]{1,0:T(8,128)S(1)}) custom-call(bf16[64,64]{1,0:T(8,128)(2,1)S(1)} %copy-done.1, s32[1,1024]{1,0:T(1,128)S(1)} %bitcast.5, s32[32,100]{1,0:T(8,128)S(1)} %copy-done.2, bf16[16384,128]{1,0:T(8,128)(2,1)S(1)} %copy-done), custom_call_target="tpu_custom_call" | custom-call | tf_op jit(solution)/shard_map/pallas_call | solution.py:227
  54.6 0.5 slice_bitcast_fusion
  55.1 0.6 %copy.7 = f32[32,100]{1,0:T(8,128)} copy(f32[32,100]{1,0:T(8,128)S(1)} %bitcast.4) | data formatting | bytes 25600
Async XLA Ops:
  0.6 2.2 %copy-start = (bf16[16384,128]{1,0:T(8,128)(2,1)S(1)}, bf16[16384,128]{1,0:T(8,128)(2,1)}, u32[]{:S(2)}) copy-start(bf16[16384,128]{1,0:T(8,128)(2,1)} %corpus_ref.1) | copy-start | bytes 12582916
  2.8 0.7 %copy-start.1 = (bf16[64,64]{1,0:T(8,128)(2,1)S(1)}, bf16[64,64]{1,0:T(8,128)(2,1)}, u32[]{:S(2)}) copy-start(bf16[64,64]{1,0:T(8,128)(2,1)} %q_ref.1) | copy-start | bytes 24580
  3.5 0.7 %copy-start.2 = (s32[32,100]{1,0:T(8,128)S(1)}, s32[32,100]{1,0:T(8,128)}, u32[]{:S(2)}) copy-start(s32[32,100]{1,0:T(8,128)} %cand_ref.1) | copy-start | bytes 38404
  4.3 0.7 %copy-start.3 = (s32[1024]{0:T(1024)S(1)}, s32[1024]{0:T(1024)}, u32[]{:S(2)}) copy-start(s32[1024]{0:T(1024)} %param.7) | copy-start | bytes 12292

commit v2 on v1

--- a/solution.py
+++ b/solution.py
@@ -9,7 +9,8 @@
 
 LANES = 128
 TILE = 256
-BLOCK = 512
+BLOCK = 4096
+STEP = 512
 MESH = pl.DeviceIdType.MESH
 
 
@@ -19,11 +20,11 @@
 
 def kernel(
     n, nf, npass_all, capacity,
-    q_ref, thr_ref, cand_ref, corpus_ref,
+    q_hbm, thr_hbm, cand_hbm, corpus_ref,
     mass_out, ans_out,
-    corpus_v, corpus_f, q_pack, q_in, q_full, cand_pad, ranks, places,
-    ids_out, ids_in, ids_sm, rows_v, vals_out, vals_in, mass_rows, mass_in,
-    load_sem, sm_sem, q_send, q_recv, ids_send, ids_recv, vals_send, vals_recv, mass_send, mass_recv,
+    q_ref, thr_ref, cand_ref, corpus_v, corpus_f, q_pack, q_in, q_full, cand_pad, places,
+    ids_out, ids_in, ids_at, ids_sm, rows_v, vals_out, vals_in, mass_rows, mass_in,
+    small_sem, load_sem, sm_sem, q_send, q_recv, ids_send, ids_recv, vals_send, vals_recv, mass_send, mass_recv,
 ):
     rows_dev, width = corpus_v.shape
     owned, per_query = cand_ref.shape
@@ -37,6 +38,11 @@
     id_bits = rows_dev.bit_length() - 1
 
     load = pltpu.make_async_copy(corpus_ref, corpus_v, load_sem)
+    small = [
+        pltpu.make_async_copy(src, dst, small_sem.at[k])
+        for k, (src, dst) in enumerate(((q_hbm, q_ref), (cand_hbm, cand_ref), (thr_hbm, thr_ref)))]
+    for copy in small:
+        copy.start()
     load.start()
 
     def tile_at(i):
@@ -56,6 +62,8 @@
         peers(i, lambda d: pl.semaphore_signal(
             barrier, inc=1, device_id=where_is(d), device_id_type=MESH))
 
+    for copy in small:
+        copy.wait()
     q_local = q_ref[...].astype(jnp.float32)
     mine = jnp.concatenate([q_local[:owned], q_local[owned:]], axis=1).astype(jnp.bfloat16)
     q_pack[...] = mine
@@ -114,14 +122,30 @@
     load.wait()
 
     def widen(b, carry):
-        at = pl.ds(pl.multiple_of(b * BLOCK, BLOCK), BLOCK)
+        at = pl.ds(pl.multiple_of(b * STEP, STEP), STEP)
         corpus_f[at, :] = corpus_v[at, :].astype(jnp.float32)
         return carry
-    lax.fori_loop(0, rows_dev // BLOCK, widen, 0)
+    lax.fori_loop(0, rows_dev // STEP, widen, 0)
 
     left = lax.broadcasted_iota(jnp.int32, (owned, LANES), 1) < half
-    to_smem = pltpu.make_async_copy(ids_in, ids_sm, sm_sem)
+    to_smem = pltpu.make_async_copy(ids_at, ids_sm, sm_sem)
     blocks = rows_dev // BLOCK
+    part = n // (2 * blocks)
+
+    def collect(source):
+        for r in range(capacity):
+            rows_v[source, pl.ds(r, 1), :] = corpus_f[pl.ds(ids_sm[source, 0, r], 1), :]
+
+    def answer(source):
+        pairs = lax.dot_general(
+            q_full[pl.ds(pl.multiple_of(source * owned, owned), owned), :],
+            rows_v[source].astype(jnp.bfloat16),
+            (((1,), (1,)), ((), ())), preferred_element_type=jnp.float32)
+        who = lax.shift_right_arithmetic(ids_in[source], jnp.int32(id_bits))
+        mask = (who == lax.broadcasted_iota(jnp.int32, (owned, LANES), 0)) & (
+            lax.broadcasted_iota(jnp.int32, (owned, LANES), 1) < capacity)
+        vals_out[source] = jnp.sum(jnp.where(mask, pairs, 0.0), axis=0, keepdims=True)
+
     for i in range(tiles):
         tile = tile_at(i)
         if i == 0:
@@ -141,6 +165,7 @@
         cutoff = thr_ref[:, pl.ds(start, TILE)].astype(jnp.float32) * 0.01
         if i == tiles - 2:
             bulk_wait(ids_in.at[pl.ds(0, n - 1)], ids_recv)
+            ids_at[...] = jnp.bitwise_and(ids_in[...], jnp.int32(rows_dev - 1))
             to_smem.start()
             to_smem.wait()
 
@@ -148,19 +173,13 @@
             at = pl.ds(pl.multiple_of(b * BLOCK, BLOCK), BLOCK)
             scores = jnp.dot(corpus_v[at, :], weights, preferred_element_type=jnp.float32)
             over = jnp.maximum(scores - cutoff, 0.0)
-            if i == tiles - 2:
-                for r in range(capacity):
-                    p = jnp.bitwise_and(ids_sm[b, 0, r], rows_dev - 1)
-                    rows_v[b, pl.ds(r, 1), :] = corpus_f[pl.ds(p, 1), :]
-            if i == tiles - 1:
-                pairs = lax.dot_general(
-                    q_full[pl.ds(pl.multiple_of(b * owned, owned), owned), :],
-                    rows_v[b].astype(jnp.bfloat16),
-                    (((1,), (1,)), ((), ())), preferred_element_type=jnp.float32)
-                who = lax.shift_right_arithmetic(ids_in[b], jnp.int32(id_bits))
-                mask = (who == lax.broadcasted_iota(jnp.int32, (owned, LANES), 0)) & (
-                    lax.broadcasted_iota(jnp.int32, (owned, LANES), 1) < capacity)
-                vals_out[b] = jnp.sum(jnp.where(mask, pairs, 0.0), axis=0, keepdims=True)
+            for k in range(part):
+                if i == tiles - 2:
+                    collect(b * part + k)
+                if i == tiles - 1:
+                    collect(n // 2 + b * part + k)
+                    answer(b * part + k)
+                    answer(n // 2 + jnp.maximum(b - 1, 0) * part + k)
             return acc + jnp.sum(over.reshape(BLOCK // 8, 8, TILE), axis=0)
 
         acc = lax.fori_loop(0, blocks, sweep, jnp.zeros((8, TILE), jnp.float32))
@@ -177,6 +196,8 @@
         if i == 0:
             mass_in[me] = mass_rows[me * owned // LANES]
 
+    for k in range(part):
+        answer(n - part + k)
     for i in range(tiles):
         def send_vals(d):
             pltpu.make_async_remote_copy(
@@ -230,17 +251,20 @@
             jax.ShapeDtypeStruct((1, LANES), jnp.float32),
             jax.ShapeDtypeStruct((owned, LANES), jnp.float32),
         ),
-        in_specs=[vmem, vmem, vmem, pl.BlockSpec(memory_space=pl.ANY)],
+        in_specs=[pl.BlockSpec(memory_space=pl.ANY)] * 4,
         out_specs=(vmem, vmem),
         scratch_shapes=[
+            pltpu.VMEM(queries.shape, jnp.bfloat16),
+            pltpu.VMEM((1, nq), jnp.int32),
+            pltpu.VMEM((owned, per_query), jnp.int32),
             pltpu.VMEM((rows_dev, width), jnp.bfloat16),
             pltpu.VMEM((rows_dev, width), jnp.float32),
             pltpu.VMEM((owned, LANES), jnp.bfloat16),
             pltpu.VMEM((n, owned, LANES), jnp.bfloat16),
             pltpu.VMEM((nq, LANES), jnp.bfloat16),
             pltpu.VMEM((owned, LANES), jnp.int32),
-            pltpu.VMEM((owned, LANES), jnp.float32),
             pltpu.VMEM((LANES, owned * LANES), jnp.bfloat16),
+            pltpu.VMEM((n, 1, LANES), jnp.int32),
             pltpu.VMEM((n, 1, LANES), jnp.int32),
             pltpu.VMEM((n, 1, LANES), jnp.int32),
             pltpu.SMEM((n, 1, LANES), jnp.int32),
@@ -249,6 +273,7 @@
             pltpu.VMEM((n, 1, LANES), jnp.float32),
             pltpu.VMEM((nq // LANES, 1, LANES), jnp.float32),
             pltpu.VMEM((n, 1, LANES), jnp.float32),
+            pltpu.SemaphoreType.DMA((3,)),
             pltpu.SemaphoreType.DMA,
             pltpu.SemaphoreType.DMA,
             pltpu.SemaphoreType.DMA,
@@ -261,7 +286,7 @@
             pltpu.SemaphoreType.DMA,
         ],
         compiler_params=pltpu.CompilerParams(
-            collective_id=0, has_side_effects=True, vmem_limit_bytes=48 * 1024 * 1024),
+            collective_id=0, has_side_effects=True),
     )(queries, threshold.reshape(1, nq), candidates, corpus)
     return mass[0, :owned], answers[:, :per_query]
 
@@ -360,7 +385,8 @@
         and n % 8 == 0
         and (n * owned) % TILE == 0
         and n * owned >= 2 * TILE
-        and rows_dev == n * BLOCK
+        and rows_dev % BLOCK == 0
+        and n % (2 * (rows_dev // BLOCK)) == 0
         and rows_dev & (rows_dev - 1) == 0
     )
     if fits:

time: 56 us -> 38.8 us (0.69)
  Pallas kernels: 49.6 us -> 35.4 us
  local copies, waits for them, and re-layouts: 5.42 us -> 2.46 us
    pallas_call x1, Pallas kernels: 49.6 us -> 35.4 us  [fused_body(): pl.pallas_call(functools.partial(kernel, n, nf, rows_dev * n, capacity),...]
    unnamed x9 -> x1, local copies, waits for them, and re-layouts: 4.91 us -> 1.32 us
    squeeze x1, local copies, waits for them, and re-layouts: 0.51 us -> 1.14 us  [fused_body(): return (mass[0, :owned], answers[:, :per_query])]
where the time goes in v2:
time: 38.8 us; the launch traced here: 38.5 us
  Pallas kernels  35.4 us (91%)
  local copies, waits for them, and re-layouts  2.46 us (6%)
  between operations  0.64 us (2%)
    pallas_call x1, Pallas kernels, fused_body(): pl.pallas_call(functools.partial(kernel, n, nf, rows_dev * n, capacity),...  35.4 us
    unnamed x1, local copies, waits for them, and re-layouts  1.32 us
    squeeze x1, local copies, waits for them, and re-layouts, fused_body(): return (mass[0, :owned], answers[:, :per_query])  1.14 us

profile of v2, /device:TPU:0, one launch (start us, length us, event | category | flops | bytes accessed | tf_op | source)
XLA Modules:
  0.0 38.5 jit_solution(18128562288415259044)
XLA Ops:
  0.6 35.4 %shard_map.59 = (f32[1,128]{1,0:T(1,128)}, f32[32,128]{1,0:T(8,128)}) custom-call(bf16[64,64]{1,0:T(8,128)(2,1)} %q_hbm.1, s32[1,1024]{1,0:T(1,128)} %bitcast.5, s32[32,100]{1,0:T(8,128)} %cand_hbm.1, bf16[16384,128]{1,0:T(8,128)(2,1)} %corpus_ref.1), custom_call_target="tpu_custom_call" | custom-call | tf_op jit(solution)/shard_map/pallas_call | solution.py:248
  36.0 1.1 %slice_bitcast_fusion = f32[32]{0:T(128)} fusion(f32[1,128]{1,0:T(1,128)} %get-tuple-element.4), kind=kLoop, calls=%fused_computation | loop fusion | bytes 256 | tf_op jit(solution)/shard_map/squeeze | solution.py:291
  37.2 1.3 %copy.7 = f32[32,100]{1,0:T(8,128)} copy(f32[32,100]{1,0:T(8,128)} %bitcast.4) | data formatting | bytes 25600

commit v3 on v2

--- a/solution.py
+++ b/solution.py
@@ -22,9 +22,9 @@
     n, nf, npass_all, capacity,
     q_hbm, thr_hbm, cand_hbm, corpus_ref,
     mass_out, ans_out,
-    q_ref, thr_ref, cand_ref, corpus_v, corpus_f, q_pack, q_in, q_full, cand_pad, places,
+    q_ref, thr_ref, cand_ref, corpus_v, corpus_f, q_pack, q_in, q_full, q_turned, cand_pad, places,
     ids_out, ids_in, ids_at, ids_sm, rows_v, vals_out, vals_in, mass_rows, mass_in,
-    small_sem, load_sem, sm_sem, q_send, q_recv, ids_send, ids_recv, vals_send, vals_recv, mass_send, mass_recv,
+    small_sem, load_sem, sm_sem, q_send, q_recv, hand_send, hand_recv, ids_send, ids_recv, vals_send, vals_recv, mass_send, mass_recv,
 ):
     rows_dev, width = corpus_v.shape
     owned, per_query = cand_ref.shape
@@ -32,10 +32,18 @@
     half = q_ref.shape[1]
     tiles = nq // TILE
     dpt = TILE // owned
-    me = lax.axis_index("rows") * nf + lax.axis_index("feat")
+    chips = n // nf
+    dpc = dpt // nf
+    core = lax.axis_index("feat")
+    me = lax.axis_index("rows") * nf + core
     my_tile = me // dpt
     my_j = me % dpt
     id_bits = rows_dev.bit_length() - 1
+    beside = my_tile + 1 - 2 * (my_tile % 2)
+    order = [beside]
+    for k in range(1, tiles // 2):
+        order += [(my_tile + 2 * k) % tiles, (beside + 2 * k) % tiles]
+    order.append(my_tile)
 
     load = pltpu.make_async_copy(corpus_ref, corpus_v, load_sem)
     small = [
@@ -45,14 +53,11 @@
         copy.start()
     load.start()
 
-    def tile_at(i):
-        return (my_tile + i) % tiles
-
     def peers(i, act):
         def step(j, carry):
-            act(tile_at(i) * dpt + (my_j + j) % dpt)
+            act(order[i] * dpt + (my_j + j) % dpt)
             return carry
-        lax.fori_loop(1 if i == 0 else 0, dpt, step, 0)
+        lax.fori_loop(1 if i == tiles - 1 else 0, dpt, step, 0, unroll=True)
 
     def where_is(d):
         return (d // nf, d % nf)
@@ -67,7 +72,8 @@
     q_local = q_ref[...].astype(jnp.float32)
     mine = jnp.concatenate([q_local[:owned], q_local[owned:]], axis=1).astype(jnp.bfloat16)
     q_pack[...] = mine
-    q_in[me] = mine
+    my_place = core * chips + me // nf
+    q_in[my_place] = mine
 
     cand_pad[...] = jnp.full(cand_pad.shape, -1, jnp.int32)
     cand_pad[:, :per_query] = cand_ref[...]
@@ -103,22 +109,6 @@
     for t in range(n):
         ids_out[t] = packed[t:t + 1]
 
-    pl.semaphore_wait(barrier, n - 1)
-
-    for i in range(tiles):
-        def send_queries(d):
-            pltpu.make_async_remote_copy(
-                src_ref=q_pack, dst_ref=q_in.at[me], send_sem=q_send, recv_sem=q_recv.at[my_tile],
-                device_id=where_is(d), device_id_type=MESH).start()
-        peers(i, send_queries)
-    for i in range(tiles):
-        def send_ids(d):
-            pltpu.make_async_remote_copy(
-                src_ref=ids_out.at[d], dst_ref=ids_in.at[me], send_sem=ids_send, recv_sem=ids_recv,
-                device_id=where_is(d), device_id_type=MESH).start()
-        peers(i, send_ids)
-    ids_in[me] = ids_out[me]
-
     load.wait()
 
     def widen(b, carry):
@@ -126,6 +116,51 @@
         corpus_f[at, :] = corpus_v[at, :].astype(jnp.float32)
         return carry
     lax.fori_loop(0, rows_dev // STEP, widen, 0)
+
+    pl.semaphore_wait(barrier, n - 1)
+
+    def send_queries(d):
+        pltpu.make_async_remote_copy(
+            src_ref=q_pack, dst_ref=q_in.at[my_place], send_sem=q_send, recv_sem=q_recv.at[my_tile],
+            device_id=where_is(d), device_id_type=MESH).start()
+
+    def send_ids(d):
+        pltpu.make_async_remote_copy(
+            src_ref=ids_out.at[d], dst_ref=ids_in.at[me], send_sem=ids_send, recv_sem=ids_recv,
+            device_id=where_is(d), device_id_type=MESH).start()
+
+    peers(0, send_queries)
+    for i in range(tiles):
+        peers(i, send_ids)
+    for i in range(1, tiles - 1):
+        for j in range(dpc):
+            send_queries((order[i] * dpc + (my_j // nf + j) % dpc) * nf + core)
+    peers(tiles - 1, send_queries)
+    ids_in[me] = ids_out[me]
+
+    def hand_over(i):
+        blocks_of = q_in.at[pl.ds(core * chips + order[i] * dpc, dpc)]
+        bulk_wait(q_in.at[pl.ds(0, dpc)], q_recv.at[order[i]])
+        pltpu.make_async_remote_copy(
+            src_ref=blocks_of, dst_ref=blocks_of, send_sem=hand_send, recv_sem=hand_recv.at[order[i]],
+            device_id=where_is(me + 1 - 2 * core), device_id_type=MESH).start()
+
+    def unpack(i):
+        if i == 0:
+            bulk_wait(q_in.at[pl.ds(0, dpt)], q_recv.at[order[i]])
+        elif i == tiles - 1:
+            bulk_wait(q_in.at[pl.ds(0, dpt - 1)], q_recv.at[order[i]])
+        else:
+            bulk_wait(q_in.at[pl.ds(0, dpc)], hand_recv.at[order[i]])
+        parts = []
+        for g in range(dpc):
+            f0 = q_in[order[i] * dpc + g].astype(jnp.float32)
+            f1 = q_in[chips + order[i] * dpc + g].astype(jnp.float32)
+            parts.append(jnp.where(left, f0, pltpu.roll(f1, half, 1)))
+            parts.append(jnp.where(left, pltpu.roll(f0, half, 1), f1))
+        asked = jnp.concatenate(parts, axis=0)
+        q_full[pl.ds(pl.multiple_of(order[i] * TILE, TILE), TILE), :] = asked.astype(jnp.bfloat16)
+        q_turned[order[i]] = asked.T.astype(jnp.bfloat16)
 
     left = lax.broadcasted_iota(jnp.int32, (owned, LANES), 1) < half
     to_smem = pltpu.make_async_copy(ids_at, ids_sm, sm_sem)
@@ -146,43 +181,44 @@
             lax.broadcasted_iota(jnp.int32, (owned, LANES), 1) < capacity)
         vals_out[source] = jnp.sum(jnp.where(mask, pairs, 0.0), axis=0, keepdims=True)
 
+    gather_first = tiles - 3
     for i in range(tiles):
-        tile = tile_at(i)
-        if i == 0:
-            bulk_wait(q_in.at[pl.ds(0, dpt - 1)], q_recv.at[tile])
-        else:
-            bulk_wait(q_in.at[pl.ds(0, dpt)], q_recv.at[tile])
-        parts = []
-        for g in range(dpt // 2):
-            f0 = q_in[tile * dpt + 2 * g].astype(jnp.float32)
-            f1 = q_in[tile * dpt + 2 * g + 1].astype(jnp.float32)
-            parts.append(jnp.where(left, f0, pltpu.roll(f1, half, 1)))
-            parts.append(jnp.where(left, pltpu.roll(f0, half, 1), f1))
-        asked = jnp.concatenate(parts, axis=0)
-        start = pl.multiple_of(tile * TILE, TILE)
-        q_full[pl.ds(start, TILE), :] = asked.astype(jnp.bfloat16)
-        weights = asked.T.astype(jnp.bfloat16)
-        cutoff = thr_ref[:, pl.ds(start, TILE)].astype(jnp.float32) * 0.01
+        tile = order[i]
+        if i < tiles - 1:
+            unpack(i)
         if i == tiles - 2:
+            unpack(tiles - 1)
+        cutoff = thr_ref[:, pl.ds(pl.multiple_of(tile * TILE, TILE), TILE)].astype(jnp.float32) * 0.01
+        if i == gather_first:
             bulk_wait(ids_in.at[pl.ds(0, n - 1)], ids_recv)
             ids_at[...] = jnp.bitwise_and(ids_in[...], jnp.int32(rows_dev - 1))
             to_smem.start()
             to_smem.wait()
 
         def sweep(b, acc):
-            at = pl.ds(pl.multiple_of(b * BLOCK, BLOCK), BLOCK)
-            scores = jnp.dot(corpus_v[at, :], weights, preferred_element_type=jnp.float32)
-            over = jnp.maximum(scores - cutoff, 0.0)
+            weights = q_turned[tile]
+            sums = []
+            for h in range(2):
+                at = pl.ds(pl.multiple_of(b * BLOCK + h * (BLOCK // 2), BLOCK // 2), BLOCK // 2)
+                scores = jnp.dot(corpus_v[at, :], weights, preferred_element_type=jnp.float32)
+                over = jnp.maximum(scores - cutoff, 0.0).reshape(BLOCK // 32, 2, 8, TILE)
+                sums.append(jnp.sum(over, axis=0))
             for k in range(part):
-                if i == tiles - 2:
+                if i == gather_first:
                     collect(b * part + k)
-                if i == tiles - 1:
+                if i == gather_first + 1:
                     collect(n // 2 + b * part + k)
                     answer(b * part + k)
                     answer(n // 2 + jnp.maximum(b - 1, 0) * part + k)
-            return acc + jnp.sum(over.reshape(BLOCK // 8, 8, TILE), axis=0)
-
-        acc = lax.fori_loop(0, blocks, sweep, jnp.zeros((8, TILE), jnp.float32))
+            return acc[0] + sums[0], acc[1] + sums[1]
+
+        zero = jnp.zeros((2, 8, TILE), jnp.float32)
+        acc = lax.fori_loop(0, blocks // 2, sweep, (zero, zero))
+        if i + 1 < tiles - 1:
+            hand_over(i + 1)
+        acc = lax.fori_loop(blocks // 2, blocks, sweep, acc)
+        acc = acc[0] + acc[1]
+        acc = acc[0] + acc[1]
         total = jnp.sum(acc, axis=0, keepdims=True)
         for h in range(TILE // LANES):
             mass_rows[tile * (TILE // LANES) + h] = total[:, h * LANES:(h + 1) * LANES]
@@ -193,18 +229,20 @@
                 send_sem=mass_send, recv_sem=mass_recv,
                 device_id=where_is(d), device_id_type=MESH).start()
         peers(i, send_mass)
-        if i == 0:
+        if i == tiles - 1:
             mass_in[me] = mass_rows[me * owned // LANES]
 
-    for k in range(part):
-        answer(n - part + k)
-    for i in range(tiles):
-        def send_vals(d):
-            pltpu.make_async_remote_copy(
-                src_ref=vals_out.at[d], dst_ref=vals_in.at[me], send_sem=vals_send, recv_sem=vals_recv,
-                device_id=where_is(d), device_id_type=MESH).start()
-        peers(i, send_vals)
-    vals_in[me] = vals_out[me]
+        if i == gather_first + 1:
+            for k in range(part):
+                answer(n - part + k)
+
+            def send_vals(d):
+                pltpu.make_async_remote_copy(
+                    src_ref=vals_out.at[d], dst_ref=vals_in.at[me], send_sem=vals_send, recv_sem=vals_recv,
+                    device_id=where_is(d), device_id_type=MESH).start()
+            for u in range(tiles):
+                peers(u, send_vals)
+            vals_in[me] = vals_out[me]
 
     bulk_wait(vals_in.at[pl.ds(0, n - 1)], vals_recv)
     values = jnp.concatenate([vals_in[t] for t in range(n)], axis=0)
@@ -233,7 +271,8 @@
         result = jnp.where(me % per_row == u, pltpu.roll(mass, LANES - u * owned, 1), result)
     mass_out[...] = result
 
-    bulk_wait(q_in.at[pl.ds(0, n - 1)], q_send)
+    bulk_wait(q_in.at[pl.ds(0, 2 * dpt - 1 + (tiles - 2) * dpc)], q_send)
+    bulk_wait(q_in.at[pl.ds(0, (tiles - 2) * dpc)], hand_send)
     bulk_wait(ids_in.at[pl.ds(0, n - 1)], ids_send)
     bulk_wait(vals_in.at[pl.ds(0, n - 1)], vals_send)
     bulk_wait(mass_in.at[pl.ds(0, n - 1)], mass_send)
@@ -262,6 +301,7 @@
             pltpu.VMEM((owned, LANES), jnp.bfloat16),
             pltpu.VMEM((n, owned, LANES), jnp.bfloat16),
             pltpu.VMEM((nq, LANES), jnp.bfloat16),
+            pltpu.VMEM((nq // TILE, LANES, TILE), jnp.bfloat16),
             pltpu.VMEM((owned, LANES), jnp.int32),
             pltpu.VMEM((LANES, owned * LANES), jnp.bfloat16),
             pltpu.VMEM((n, 1, LANES), jnp.int32),
@@ -276,6 +316,8 @@
             pltpu.SemaphoreType.DMA((3,)),
             pltpu.SemaphoreType.DMA,
             pltpu.SemaphoreType.DMA,
+            pltpu.SemaphoreType.DMA,
+            pltpu.SemaphoreType.DMA((nq // TILE,)),
             pltpu.SemaphoreType.DMA,
             pltpu.SemaphoreType.DMA((nq // TILE,)),
             pltpu.SemaphoreType.DMA,
@@ -384,7 +426,7 @@
         and capacity <= LANES
         and n % 8 == 0
         and (n * owned) % TILE == 0
-        and n * owned >= 2 * TILE
+        and n * owned == 4 * TILE
         and rows_dev % BLOCK == 0
         and n % (2 * (rows_dev // BLOCK)) == 0
         and rows_dev & (rows_dev - 1) == 0

time: 38.8 us -> 34.6 us (0.89)
  Pallas kernels: 35.4 us -> 31.1 us
    pallas_call x1, Pallas kernels: 35.4 us -> 31.1 us  [fused_body(): pl.pallas_call(functools.partial(kernel, n, nf, rows_dev * n, capacity),...]
where the time goes in v3:
time: 34.6 us; the launch traced here: 34.2 us
  Pallas kernels  31.1 us (90%)
  local copies, waits for them, and re-layouts  2.46 us (7%)
  between operations  0.64 us (2%)
    pallas_call x1, Pallas kernels, fused_body(): pl.pallas_call(functools.partial(kernel, n, nf, rows_dev * n, capacity),...  31.1 us
    unnamed x1, local copies, waits for them, and re-layouts  1.32 us
    squeeze x1, local copies, waits for them, and re-layouts, fused_body(): return (mass[0, :owned], answers[:, :per_query])  1.14 us

profile of v3, /device:TPU:0, one launch (start us, length us, event | category | flops | bytes accessed | tf_op | source)
XLA Modules:
  0.0 34.2 jit_solution(6526314250511320775)
XLA Ops:
  0.6 31.1 %shard_map.59 = (f32[1,128]{1,0:T(1,128)}, f32[32,128]{1,0:T(8,128)}) custom-call(bf16[64,64]{1,0:T(8,128)(2,1)} %q_hbm.1, s32[1,1024]{1,0:T(1,128)} %bitcast.5, s32[32,100]{1,0:T(8,128)} %cand_hbm.1, bf16[16384,128]{1,0:T(8,128)(2,1)} %corpus_ref.1), custom_call_target="tpu_custom_call" | custom-call | tf_op jit(solution)/shard_map/pallas_call | solution.py:287
  31.7 1.1 %slice_bitcast_fusion = f32[32]{0:T(128)} fusion(f32[1,128]{1,0:T(1,128)} %get-tuple-element.4), kind=kLoop, calls=%fused_computation | loop fusion | bytes 256 | tf_op jit(solution)/shard_map/squeeze | solution.py:333
  32.9 1.3 %copy.7 = f32[32,100]{1,0:T(8,128)} copy(f32[32,100]{1,0:T(8,128)} %bitcast.4) | data formatting | bytes 25600

commit v4 on v3

--- a/solution.py
+++ b/solution.py
@@ -24,7 +24,7 @@
     mass_out, ans_out,
     q_ref, thr_ref, cand_ref, corpus_v, corpus_f, q_pack, q_in, q_full, q_turned, cand_pad, places,
     ids_out, ids_in, ids_at, ids_sm, rows_v, vals_out, vals_in, mass_rows, mass_in,
-    small_sem, load_sem, sm_sem, q_send, q_recv, hand_send, hand_recv, ids_send, ids_recv, vals_send, vals_recv, mass_send, mass_recv,
+    small_sem, load_sem, sm_sem, q_send, q_recv, hand_send, hand_recv, far_sem, ids_send, ids_recv, vals_send, vals_recv, mass_send, mass_recv,
 ):
     rows_dev, width = corpus_v.shape
     owned, per_query = cand_ref.shape
@@ -63,9 +63,18 @@
         return (d // nf, d % nf)
 
     barrier = pltpu.get_barrier_semaphore()
-    for i in range(tiles):
-        peers(i, lambda d: pl.semaphore_signal(
-            barrier, inc=1, device_id=where_is(d), device_id_type=MESH))
+    inner = (my_tile >= 1) & (my_tile < tiles - 1)
+    across = (tiles - 1 - my_tile) * dpt + my_j
+    nearby = beside * dpt + my_j
+
+    def signal(sem, d):
+        pl.semaphore_signal(sem, inc=1, device_id=where_is(d), device_id_type=MESH)
+
+    @pl.when(inner)
+    def _():
+        signal(barrier, across)
+    peers(0, functools.partial(signal, barrier))
+    peers(tiles - 1, functools.partial(signal, barrier))
 
     for copy in small:
         copy.wait()
@@ -117,7 +126,13 @@
         return carry
     lax.fori_loop(0, rows_dev // STEP, widen, 0)
 
-    pl.semaphore_wait(barrier, n - 1)
+    @pl.when(inner)
+    def _():
+        pl.semaphore_wait(barrier, 2 * dpt)
+
+    @pl.when(jnp.logical_not(inner))
+    def _():
+        pl.semaphore_wait(barrier, 2 * dpt - 1)
 
     def send_queries(d):
         pltpu.make_async_remote_copy(
@@ -129,8 +144,18 @@
             src_ref=ids_out.at[d], dst_ref=ids_in.at[me], send_sem=ids_send, recv_sem=ids_recv,
             device_id=where_is(d), device_id_type=MESH).start()
 
+    @pl.when(inner)
+    def _():
+        signal(far_sem, across)
     peers(0, send_queries)
-    for i in range(tiles):
+    peers(0, send_ids)
+    peers(tiles - 1, send_ids)
+    pl.semaphore_wait(far_sem, 1)
+
+    @pl.when(inner)
+    def _():
+        signal(far_sem, nearby)
+    for i in range(1, tiles - 1):
         peers(i, send_ids)
     for i in range(1, tiles - 1):
         for j in range(dpc):
@@ -320,6 +345,7 @@
             pltpu.SemaphoreType.DMA((nq // TILE,)),
             pltpu.SemaphoreType.DMA,
             pltpu.SemaphoreType.DMA((nq // TILE,)),
+            pltpu.SemaphoreType.REGULAR,
             pltpu.SemaphoreType.DMA,
             pltpu.SemaphoreType.DMA,
             pltpu.SemaphoreType.DMA,

time: 34.6 us -> 32.5 us (0.939)
  Pallas kernels: 31.1 us -> 29 us
    pallas_call x1, Pallas kernels: 31.1 us -> 29 us  [fused_body(): pl.pallas_call(functools.partial(kernel, n, nf, rows_dev * n, capacity),...]
where the time goes in v4:
time: 32.5 us; the launch traced here: 32.1 us
  Pallas kernels  29 us (89%)
  local copies, waits for them, and re-layouts  2.46 us (8%)
  between operations  0.64 us (2%)
    pallas_call x1, Pallas kernels, fused_body(): pl.pallas_call(functools.partial(kernel, n, nf, rows_dev * n, capacity),...  29 us
    unnamed x1, local copies, waits for them, and re-layouts  1.32 us
    squeeze x1, local copies, waits for them, and re-layouts, fused_body(): return (mass[0, :owned], answers[:, :per_query])  1.14 us

profile of v4, /device:TPU:0, one launch (start us, length us, event | category | flops | bytes accessed | tf_op | source)
XLA Modules:
  0.0 32.1 jit_solution(8750654752941907068)
XLA Ops:
  0.6 29.0 %shard_map.59 = (f32[1,128]{1,0:T(1,128)}, f32[32,128]{1,0:T(8,128)}) custom-call(bf16[64,64]{1,0:T(8,128)(2,1)} %q_hbm.1, s32[1,1024]{1,0:T(1,128)} %bitcast.5, s32[32,100]{1,0:T(8,128)} %cand_hbm.1, bf16[16384,128]{1,0:T(8,128)(2,1)} %corpus_ref.1), custom_call_target="tpu_custom_call" | custom-call | tf_op jit(solution)/shard_map/pallas_call | solution.py:312
  29.7 1.1 %slice_bitcast_fusion = f32[32]{0:T(128)} fusion(f32[1,128]{1,0:T(1,128)} %get-tuple-element.4), kind=kLoop, calls=%fused_computation | loop fusion | bytes 256 | tf_op jit(solution)/shard_map/squeeze | solution.py:359
  30.8 1.3 %copy.7 = f32[32,100]{1,0:T(8,128)} copy(f32[32,100]{1,0:T(8,128)} %bitcast.4) | data formatting | bytes 25600

commit v5 on v4

--- a/solution.py
+++ b/solution.py
@@ -10,6 +10,7 @@
 LANES = 128
 TILE = 256
 BLOCK = 4096
+MIXED = 2048
 STEP = 512
 MESH = pl.DeviceIdType.MESH
 
@@ -148,6 +149,7 @@
     def _():
         signal(far_sem, across)
     peers(0, send_queries)
+    peers(tiles - 1, send_queries)
     peers(0, send_ids)
     peers(tiles - 1, send_ids)
     pl.semaphore_wait(far_sem, 1)
@@ -160,7 +162,6 @@
     for i in range(1, tiles - 1):
         for j in range(dpc):
             send_queries((order[i] * dpc + (my_j // nf + j) % dpc) * nf + core)
-    peers(tiles - 1, send_queries)
     ids_in[me] = ids_out[me]
 
     def hand_over(i):
@@ -189,8 +190,8 @@
 
     left = lax.broadcasted_iota(jnp.int32, (owned, LANES), 1) < half
     to_smem = pltpu.make_async_copy(ids_at, ids_sm, sm_sem)
-    blocks = rows_dev // BLOCK
-    part = n // (2 * blocks)
+    gather_tile = tiles - 2
+    part = n // (rows_dev // MIXED)
 
     def collect(source):
         for r in range(capacity):
@@ -206,41 +207,39 @@
             lax.broadcasted_iota(jnp.int32, (owned, LANES), 1) < capacity)
         vals_out[source] = jnp.sum(jnp.where(mask, pairs, 0.0), axis=0, keepdims=True)
 
-    gather_first = tiles - 3
+    unpack(tiles - 1)
     for i in range(tiles):
         tile = order[i]
         if i < tiles - 1:
             unpack(i)
-        if i == tiles - 2:
-            unpack(tiles - 1)
+        size = MIXED if i == gather_tile else BLOCK
+        blocks = rows_dev // size
         cutoff = thr_ref[:, pl.ds(pl.multiple_of(tile * TILE, TILE), TILE)].astype(jnp.float32) * 0.01
-        if i == gather_first:
-            bulk_wait(ids_in.at[pl.ds(0, n - 1)], ids_recv)
-            ids_at[...] = jnp.bitwise_and(ids_in[...], jnp.int32(rows_dev - 1))
-            to_smem.start()
+        if i == gather_tile:
             to_smem.wait()
 
         def sweep(b, acc):
             weights = q_turned[tile]
             sums = []
             for h in range(2):
-                at = pl.ds(pl.multiple_of(b * BLOCK + h * (BLOCK // 2), BLOCK // 2), BLOCK // 2)
+                at = pl.ds(pl.multiple_of(b * size + h * (size // 2), size // 2), size // 2)
                 scores = jnp.dot(corpus_v[at, :], weights, preferred_element_type=jnp.float32)
-                over = jnp.maximum(scores - cutoff, 0.0).reshape(BLOCK // 32, 2, 8, TILE)
+                over = jnp.maximum(scores - cutoff, 0.0).reshape(size // 32, 2, 8, TILE)
                 sums.append(jnp.sum(over, axis=0))
-            for k in range(part):
-                if i == gather_first:
+            if i == gather_tile:
+                for k in range(part):
                     collect(b * part + k)
-                if i == gather_first + 1:
-                    collect(n // 2 + b * part + k)
-                    answer(b * part + k)
-                    answer(n // 2 + jnp.maximum(b - 1, 0) * part + k)
+                    answer(jnp.maximum(b - 1, 0) * part + k)
             return acc[0] + sums[0], acc[1] + sums[1]
 
         zero = jnp.zeros((2, 8, TILE), jnp.float32)
         acc = lax.fori_loop(0, blocks // 2, sweep, (zero, zero))
         if i + 1 < tiles - 1:
             hand_over(i + 1)
+        if i == gather_tile - 1:
+            bulk_wait(ids_in.at[pl.ds(0, n - 1)], ids_recv)
+            ids_at[...] = jnp.bitwise_and(ids_in[...], jnp.int32(rows_dev - 1))
+            to_smem.start()
         acc = lax.fori_loop(blocks // 2, blocks, sweep, acc)
         acc = acc[0] + acc[1]
         acc = acc[0] + acc[1]
@@ -257,7 +256,7 @@
         if i == tiles - 1:
             mass_in[me] = mass_rows[me * owned // LANES]
 
-        if i == gather_first + 1:
+        if i == gather_tile:
             for k in range(part):
                 answer(n - part + k)
 
@@ -454,7 +453,8 @@
         and (n * owned) % TILE == 0
         and n * owned == 4 * TILE
         and rows_dev % BLOCK == 0
-        and n % (2 * (rows_dev // BLOCK)) == 0
+        and n % (rows_dev // MIXED) == 0
+        and rows_dev % (2 * BLOCK) == 0
         and rows_dev & (rows_dev - 1) == 0
     )
     if fits:

time: 32.5 us -> 31.3 us (0.963)
  Pallas kernels: 29 us -> 27.8 us
    pallas_call x1, Pallas kernels: 29 us -> 27.8 us  [fused_body(): pl.pallas_call(functools.partial(kernel, n, nf, rows_dev * n, capacity),...]
where the time goes in v5:
time: 31.3 us; the launch traced here: 30.9 us
  Pallas kernels  27.8 us (89%)
  local copies, waits for them, and re-layouts  2.46 us (8%)
  between operations  0.64 us (2%)
    pallas_call x1, Pallas kernels, fused_body(): pl.pallas_call(functools.partial(kernel, n, nf, rows_dev * n, capacity),...  27.8 us
    unnamed x1, local copies, waits for them, and re-layouts  1.32 us
    squeeze x1, local copies, waits for them, and re-layouts, fused_body(): return (mass[0, :owned], answers[:, :per_query])  1.14 us

profile of v5, /device:TPU:0, one launch (start us, length us, event | category | flops | bytes accessed | tf_op | source)
XLA Modules:
  0.0 30.9 jit_solution(425735622585640767)
XLA Ops:
  0.6 27.8 %shard_map.59 = (f32[1,128]{1,0:T(1,128)}, f32[32,128]{1,0:T(8,128)}) custom-call(bf16[64,64]{1,0:T(8,128)(2,1)} %q_hbm.1, s32[1,1024]{1,0:T(1,128)} %bitcast.5, s32[32,100]{1,0:T(8,128)} %cand_hbm.1, bf16[16384,128]{1,0:T(8,128)(2,1)} %corpus_ref.1), custom_call_target="tpu_custom_call" | custom-call | tf_op jit(solution)/shard_map/pallas_call | solution.py:311
  28.5 1.1 %slice_bitcast_fusion = f32[32]{0:T(128)} fusion(f32[1,128]{1,0:T(1,128)} %get-tuple-element.4), kind=kLoop, calls=%fused_computation | loop fusion | bytes 256 | tf_op jit(solution)/shard_map/squeeze | solution.py:358
  29.6 1.3 %copy.7 = f32[32,100]{1,0:T(8,128)} copy(f32[32,100]{1,0:T(8,128)} %bitcast.4) | data formatting | bytes 25600
